TPU v7x, 256 devices: a whole 4x4x8 slice. The times are simulated.
256 devices in a mesh: level: 4 (over y), blk: 64 (over x, z, core).
Axes of the slice: x: 4, y: 4, z: 8, core: 2. Of those that a mesh axis runs over, the one named last changes fastest.
Arguments:
- right_sides: float32 [4, 512, 16384], P('level', None, 'blk'), may hold values from -6 to 6
- leaf_gen: float32 [4, 16384, 256], P('level', 'blk'), may hold values from -1 to 1, as said below
- leaf_inverse: float32 [4, 8192, 128], P('level', 'blk'), may hold values from -0.5 to 0.5
- leaf_lower: float32 [4, 8192, 128], P('level', 'blk'), may hold values from -0.5 to 0.5
- node_gen: float32 [4, 64, 6, 256, 256], P('level', 'blk'), may hold values from -1 to 1, as said below
- node_inverse: float32 [4, 64, 6, 128, 128], P('level', 'blk'), may hold values from -1 to 1, as said below
- node_lower: float32 [4, 64, 6, 128, 128], P('level', 'blk'), may hold values from -1 to 1, as said below
- coupling: float32 [4, 128, 256], P('level'), may hold values from -0.5 to 0.5
- child_leaf: int32 [4], P('level'), may hold values from 0 to 63
Outputs:
- leaf_solution: float32 [4, 512, 8192], P('level', None, 'blk')
- node_solution: float32 [4, 64, 6, 512, 128], P('level', 'blk')
- root_skeleton: float32 [4, 512, 128], P('level')
Inputs may be any that keep to these rules, and one draw needn't show every extreme that they name: `leaf_gen`: each leaf's 256 x 256 block is orthogonal. node_gen[p, i, h] is orthogonal and equal for all leaves i with the same i >> (h + 1). node_inverse[p, i, h] is equal for all leaves i with the same i >> (h + 1). node_lower[p, i, h] is equal for all leaves i with the same i >> (h + 1).
All inputs are finite; a program needn't handle non-finite values.
Results may differ from a plain program's by a relative error of at most 0.0003.
Values sent between devices are 32-bit elements; how exact they have to be, the bound alone decides.
A program may use at most 64 MiB of HBM per device.

v0:
```python
import jax
import jax.numpy as jnp
from jax import lax
from jax.sharding import Mesh
from jax.sharding import PartitionSpec as P

BLK = ("blk_0", "blk_1", "blk_2")


exact_mode = lax.Precision.HIGHEST


def partner_2(value, axis, distance):
    mask = 2**distance
    pairs = [(source, source ^ mask) for source in range(lax.axis_size(axis))]
    return lax.ppermute(value, axis, pairs)


def from_root(value, axes, root):
    value = jnp.where(lax.axis_index(axes) == root, value, jnp.zeros_like(value))
    for axis in axes:
        value = lax.psum(value, axis)
    return value


def in_one_piece(arrays, axis, dim, along):
    widths = [a.shape[along] for a in arrays]
    both = jnp.concatenate(arrays, axis=along)
    out = lax.all_gather(both, axis, axis=dim, tiled=True)
    return tuple(jnp.split(out, [sum(widths[:k]) for k in range(1, len(widths))], axis=along))


def product(left, right):
    return jnp.matmul(left, right, precision=exact_mode)


def solve_front(
    columns, position, leaf_gen, leaf_inverse, leaf_lower, node_gen, node_inverse, node_lower
):
    redundant = leaf_inverse.shape[2]
    skeleton_size = leaf_lower.shape[2]
    height = node_gen.shape[2]
    turned = product(columns, leaf_gen[0])
    solved = product(turned[:, :redundant], leaf_inverse[0])
    skeleton = turned[:, redundant:] - product(solved, leaf_lower[0])
    node_parts = []
    for tier_index in range(height):
        payload = skeleton
        both = partner_2(payload, BLK, tier_index)
        is_upper = position >> tier_index & 1 == 1
        joined = jnp.where(
            is_upper,
            jnp.concatenate([both, skeleton], axis=1),
            jnp.concatenate([skeleton, both], axis=1),
        )
        generator = node_gen[0, 0, tier_index]
        turned_node = product(joined, generator)
        node_solved = product(turned_node[:, :skeleton_size], node_inverse[0, 0, tier_index])
        skeleton = turned_node[:, skeleton_size:] - product(
            node_solved, node_lower[0, 0, tier_index]
        )
        node_parts.append(node_solved)
    return (solved, jnp.stack(node_parts), skeleton)


def compose_maps(
    position, coupling, leaf_gen, leaf_inverse, leaf_lower, node_gen, node_inverse, node_lower
):
    redundant = leaf_inverse.shape[2]
    skeleton_size = leaf_lower.shape[2]
    height = node_gen.shape[2]
    lifted = product(coupling[0], leaf_gen[0])
    leaf_map = product(lifted[:, :redundant], leaf_inverse[0])
    carried = lifted[:, redundant:] - product(leaf_map, leaf_lower[0])
    tier_maps = []
    for tier_index in range(height):
        is_upper = position >> tier_index & 1 == 1
        generator = node_gen[0, 0, tier_index]
        half_rows = jnp.where(is_upper, generator[skeleton_size:], generator[:skeleton_size])
        turned = product(carried, half_rows)
        node_map = product(turned[:, :skeleton_size], node_inverse[0, 0, tier_index])
        carried = turned[:, skeleton_size:] - product(node_map, node_lower[0, 0, tier_index])
        tier_maps.append(node_map)
    return (leaf_map, jnp.stack(tier_maps), carried)


def shards(
    right_sides,
    leaf_gen,
    leaf_inverse,
    leaf_lower,
    node_gen,
    node_inverse,
    node_lower,
    coupling,
    child_leaf,
):
    column_total = right_sides.shape[1]
    skeleton_size = leaf_lower.shape[2]
    height = node_gen.shape[2]
    level_index = lax.axis_index("level")
    position = lax.axis_index(BLK)
    is_target = position == child_leaf[0]
    tiers = jnp.arange(height, dtype=jnp.int32)
    in_subtree = (position >> tiers + 1 == child_leaf[0] >> tiers + 1)[:, None, None]
    solved, stacked, skeleton = solve_front(
        right_sides[0],
        position,
        leaf_gen,
        leaf_inverse,
        leaf_lower,
        node_gen,
        node_inverse,
        node_lower,
    )
    leaf_map, tier_maps, root_map = compose_maps(
        position, coupling, leaf_gen, leaf_inverse, leaf_lower, node_gen, node_inverse, node_lower
    )
    tier_maps, root_map = (
        from_root(tier_maps, BLK, child_leaf[0]),
        from_root(root_map, BLK, child_leaf[0]),
    )
    all_maps, all_roots = in_one_piece((root_map[None], skeleton[None]), "level", 0, 1)

    def advance(earlier, paired):
        latest = paired[1] + product(earlier, paired[0])
        return (latest, earlier)

    final_root, incomings = lax.scan(
        advance, jnp.zeros((column_total, skeleton_size), jnp.float32), (all_maps, all_roots)
    )
    incoming = lax.dynamic_index_in_dim(incomings, level_index, 0, keepdims=False)
    leaf_part = solved + jnp.where(is_target, product(incoming, leaf_map), 0.0)
    node_part = stacked + jnp.where(in_subtree, product(incoming[None], tier_maps), 0.0)
    root_part = skeleton + product(incoming, root_map)
    return (leaf_part[None], node_part[None, None], root_part[None])


def solution(mesh):
    split = Mesh(
        mesh.devices.reshape(mesh.shape["level"], 4, 8, 2), ("level", "blk_0", "blk_1", "blk_2")
    )
    return jax.shard_map(
        shards,
        mesh=split,
        in_specs=(
            P("level", None, BLK),
            P("level", BLK, None),
            P("level", BLK, None),
            P("level", BLK, None),
            P("level", BLK, None, None, None),
            P("level", BLK, None, None, None),
            P("level", BLK, None, None, None),
            P("level", None, None),
            P("level"),
        ),
        out_specs=(
            P("level", None, BLK),
            P("level", BLK, None, None, None),
            P("level", None, None),
        ),
        check_vma=False,
    )
```

profile of v0, /device:TPU:27, one launch (start us, length us, event | category | flops | bytes accessed | tf_op | source)
XLA Modules:
  0.0 275.7 jit_solution(7446985248511969324)
XLA Ops:
  7.3 1.0 copy-done
  8.3 1.6 fusion.49
  9.9 1.5 fusion.63
  11.4 1.1 convolution_subtract_fusion
  12.5 0.7 collective-permute-start
  13.2 1.2 fusion.74
  14.9 0.3 fusion.102
  15.2 1.7 bitcast_dynamic-update-slice_fusion.12
  17.1 0.3 fusion.100
  17.3 0.8 bitcast_dynamic-update-slice_fusion.11
  18.4 0.3 fusion.98
  18.6 0.8 bitcast_dynamic-update-slice_fusion.10
  19.7 0.3 fusion.96
  19.9 0.8 bitcast_dynamic-update-slice_fusion.9
  21.0 0.3 fusion.94
  21.3 1.9 fusion.13
  23.2 2.1 bitcast_dynamic-update-slice_fusion.6
  25.3 1.1 slice_subtract_fusion.5
  26.4 1.6 collective-permute-start.1
  28.0 1.7 bitcast_dynamic-update-slice_fusion.8
  29.9 5.0 %collective-permute-done.1 = f32[512,128]{0,1:T(8,128)} collective-permute-done((f32[512,128]{0,1:T(8,128)}, f32[512,128]{0,1:T(8,128)}, u32[]{:S(2)}, u32[]{:S(2)}) %collective-permute-start.1) | collective-permute-done | bytes 262176 | tf_op jit(solution)/shard_map/ppermute | solution.py:16
  34.9 1.9 fusion.19
  36.8 2.1 bitcast_dynamic-update-slice_fusion.5
  38.9 1.1 slice_subtract_fusion.4
  40.0 3.0 %collective-permute-start.2 = (f32[512,128]{0,1:T(8,128)}, f32[512,128]{0,1:T(8,128)}, u32[]{:S(2)}, u32[]{:S(2)}) collective-permute-start(f32[512,128]{0,1:T(8,128)} %slice_subtract_fusion.4), channel_id=1, source_target_pairs={{0,4},{1,5},{2,6},{3,7},{4,0},{5,1},{6,2},{7,3},{8,12},{9,13},{10,... | collective-permute-start | bytes 786440 | tf_op jit(solution)/shard_map/ppermute | solution.py:16
  43.0 0.3 fusion.92
  44.0 1.7 bitcast_dynamic-update-slice_fusion.7
  45.7 9.3 %collective-permute-done.2 = f32[512,128]{0,1:T(8,128)} collective-permute-done((f32[512,128]{0,1:T(8,128)}, f32[512,128]{0,1:T(8,128)}, u32[]{:S(2)}, u32[]{:S(2)}) %collective-permute-start.2) | collective-permute-done | bytes 262176 | tf_op jit(solution)/shard_map/ppermute | solution.py:16
  54.9 1.9 fusion.25
  56.8 2.1 bitcast_dynamic-update-slice_fusion.4
  59.0 1.1 slice_subtract_fusion.3
  60.1 6.2 %collective-permute-start.3 = (f32[512,128]{0,1:T(8,128)}, f32[512,128]{0,1:T(8,128)}, u32[]{:S(2)}, u32[]{:S(2)}) collective-permute-start(f32[512,128]{0,1:T(8,128)} %slice_subtract_fusion.3), channel_id=1, source_target_pairs={{0,8},{1,9},{2,10},{3,11},{4,12},{5,13},{6,14},{7,15},{8,0},{9,1},... | collective-permute-start | bytes 786440 | tf_op jit(solution)/shard_map/ppermute | solution.py:16
  66.3 0.8 fusion.12
  67.2 0.8 broadcast_select_fusion
  68.2 7.1 %collective-permute-done.3 = f32[512,128]{0,1:T(8,128)} collective-permute-done((f32[512,128]{0,1:T(8,128)}, f32[512,128]{0,1:T(8,128)}, u32[]{:S(2)}, u32[]{:S(2)}) %collective-permute-start.3) | collective-permute-done | bytes 262176 | tf_op jit(solution)/shard_map/ppermute | solution.py:16
  75.3 1.9 fusion.31
  77.1 2.1 bitcast_dynamic-update-slice_fusion.3
  79.3 1.1 slice_subtract_fusion.2
  80.4 0.3 collective-permute-start.4
  80.7 30.9 %all-reduce.9.cloned.1.call-done = (f32[128,128]{1,0:T(8,128)}, f32[6,128,128]{2,1,0:T(8,128)}) async-done(((f32[128,128]{1,0:T(8,128)}, f32[6,128,128]{2,1,0:T(8,128)}), (f32[128,128]{1,0:T(8,128)}, f32[6,128,128]{2,1,0:T(8,128)})) %all-reduce.9.cloned.1.call-update) | async-done | bytes 458768 | tf_op jit(solution)/shard_map/psum | solution.py:22
  111.7 1.9 fusion.37
  113.5 2.1 bitcast_dynamic-update-slice_fusion.2
  115.7 1.1 slice_subtract_fusion.1
  116.8 1.7 collective-permute-start.5
  118.5 67.4 %all-reduce.7.cloned.1.call-done = (f32[128,128]{1,0:T(8,128)}, f32[6,128,128]{2,1,0:T(8,128)}) async-done(((f32[128,128]{1,0:T(8,128)}, f32[6,128,128]{2,1,0:T(8,128)}), (f32[128,128]{1,0:T(8,128)}, f32[6,128,128]{2,1,0:T(8,128)})) %all-reduce.7.cloned.1.call-update) | async-done | bytes 458768 | tf_op jit(solution)/shard_map/psum | solution.py:22
  186.0 2.0 fusion.43
  188.1 1.9 bitcast_dynamic-update-slice_fusion.1
  190.0 1.2 fusion.138
  191.2 30.8 %all-reduce.11.cloned.1.call-done = (f32[128,128]{1,0:T(8,128)}, f32[6,128,128]{2,1,0:T(8,128)}) async-done(((f32[128,128]{1,0:T(8,128)}, f32[6,128,128]{2,1,0:T(8,128)}), (f32[128,128]{1,0:T(8,128)}, f32[6,128,128]{2,1,0:T(8,128)})) %all-reduce.11.cloned.1.call-update) | async-done | bytes 458768 | tf_op jit(solution)/shard_map/psum | solution.py:22
  222.0 1.6 pad_maximum_fusion
  223.7 26.2 %all-gather.2.cloned.1.call-done = f32[4,640,128]{2,1,0:T(8,128)} async-done(((f32[1,640,128]{2,1,0:T(8,128)}), f32[4,640,128]{2,1,0:T(8,128)}) %all-gather.2.cloned.1.call-update) | async-done | bytes 1310736 | tf_op jit(solution)/shard_map/all_gather | solution.py:29
  249.9 1.8 split.9
  251.7 8.8 %while.13 = (s32[]{:T(128)}, f32[512,128]{0,1:T(8,128)S(1)}, f32[4,512,128]{1,2,0:T(8,128)}, f32[4,512,128]{2,1,0:T(8,128)S(1)}, f32[4,128,128]{2,1,0:T(8,128)}, /*index=5*/s32[]{:T(128)}, s32[]{:T(128)}) while((s32[]{:T(128)}, f32[512,128]{0,1:T(8,128)S(1)}, f32[4,512,128]{1,2,0:T(8,128)}, f32[4,512,128]{2,1,0:T(8,128)S(1)}, ...), condition=%wide.region_4.5_spmd.clone, body=%wide.region_3.4_spmd.clone.sunk | while | flops 100859904 | bytes 2949228 | solution.py:129
  251.9 0.7 bitcast_dynamic-update-slice_fusion.14
  252.6 1.3 fusion.249
  254.1 0.7 bitcast_dynamic-update-slice_fusion.14
  254.8 1.3 fusion.249
  256.3 0.7 bitcast_dynamic-update-slice_fusion.14
  257.0 1.3 fusion.249
  258.5 0.7 bitcast_dynamic-update-slice_fusion.14
  259.2 1.3 fusion.249
  260.5 2.3 fusion.9
  262.8 2.2 fusion.11
  265.1 4.1 %fusion.8 = f32[1,1,6,512,128]{4,3,2,1,0:T(8,128)} fusion(f32[6,512,128]{2,1,0:T(8,128)} %get-tuple-element.97, f32[6,128,128]{2,1,0:T(8,128)S(1)} %copy-done.4, pred[6]{0:T(512)(128)(4,1)S(1)} %shift-right-arithmetic_compare_fusion, f32[4,512,128]{1,2,0:T(8,128)} %get-tuple-element.30, s32[]{:T(128)S(6)} %select_n.162), kind=kOutput, calls=%fused_computation.12 | convolution fusion | flops 604766208 | bytes 3801098 | tf_op jit(solution)/shard_map/dot_general | solution.py:34
  (53 shorter events, 2.6 us)
Async XLA Ops:
  7.2 1.1 copy-start
  7.2 7.3 %copy-start.5 = (f32[1,128,128]{2,1,0:T(8,128)S(1)}, f32[1,128,128]{2,1,0:T(8,128)}, u32[]{:S(2)}) copy-start(f32[1,128,128]{2,1,0:T(8,128)} %param.13) | copy-start | bytes 196612
  7.2 4.2 %copy-start.7 = (f32[1,128,128]{2,1,0:T(8,128)S(1)}, f32[1,128,128]{2,1,0:T(8,128)}, u32[]{:S(2)}) copy-start(f32[1,128,128]{2,1,0:T(8,128)} %param.14) | copy-start | bytes 196612
  7.2 6.0 %copy-start.8 = (f32[1,128,256]{2,1,0:T(8,128)S(1)}, f32[1,128,256]{2,1,0:T(8,128)}, u32[]{:S(2)}) copy-start(f32[1,128,256]{2,1,0:T(8,128)} %param.18) | copy-start | bytes 393220
  7.2 7.7 %copy-start.1 = (f32[1,1,6,256,256]{4,3,2,1,0:T(8,128)S(1)}, f32[1,1,6,256,256]{4,3,2,1,0:T(8,128)}, u32[]{:S(2)}) copy-start(f32[1,1,6,256,256]{4,3,2,1,0:T(8,128)} %param.15) | copy-start | bytes 4718596
  7.2 104.4 %all-reduce.9.cloned.1.call-start = ((), (), s32[]{:S(2)}) async-start(), calls=%async_computation.2 | async-start | bytes 917504 | tf_op jit(solution)/shard_map/psum | solution.py:22
  9.9 6.9 %copy-start.2 = (f32[1,1,6,128,128]{4,3,2,1,0:T(8,128)S(1)}, f32[1,1,6,128,128]{4,3,2,1,0:T(8,128)}, u32[]{:S(2)}) copy-start(f32[1,1,6,128,128]{4,3,2,1,0:T(8,128)} %param.17) | copy-start | bytes 1179652
  12.5 4.8 %copy-start.3 = (f32[1,1,6,128,128]{4,3,2,1,0:T(8,128)S(1)}, f32[1,1,6,128,128]{4,3,2,1,0:T(8,128)}, u32[]{:S(2)}) copy-start(f32[1,1,6,128,128]{4,3,2,1,0:T(8,128)} %param.16) | copy-start | bytes 1179652
  12.5 8.7 %collective-permute-start = (f32[512,128]{0,1:T(8,128)}, f32[512,128]{0,1:T(8,128)}, u32[]{:S(2)}, u32[]{:S(2)}) collective-permute-start(f32[512,128]{0,1:T(8,128)} %convolution_subtract_fusion), channel_id=1, source_target_pairs={{0,1},{1,0},{2,3},{3,2},{4,5},{5,4},{6,7},{7,6},{8,9},{9,8},{10,11... | collective-permute-start | bytes 786440 | tf_op jit(solution)/shard_map/ppermute | solution.py:16
  26.4 8.5 %collective-permute-start.1 = (f32[512,128]{0,1:T(8,128)}, f32[512,128]{0,1:T(8,128)}, u32[]{:S(2)}, u32[]{:S(2)}) collective-permute-start(f32[512,128]{0,1:T(8,128)} %slice_subtract_fusion.5), channel_id=1, source_target_pairs={{0,2},{1,3},{2,0},{3,1},{4,6},{5,7},{6,4},{7,5},{8,10},{9,11},{10,... | collective-permute-start | bytes 786440 | tf_op jit(solution)/shard_map/ppermute | solution.py:16
  40.0 14.9 %collective-permute-start.2 = (f32[512,128]{0,1:T(8,128)}, f32[512,128]{0,1:T(8,128)}, u32[]{:S(2)}, u32[]{:S(2)}) collective-permute-start(f32[512,128]{0,1:T(8,128)} %slice_subtract_fusion.4), channel_id=1, source_target_pairs={{0,4},{1,5},{2,6},{3,7},{4,0},{5,1},{6,2},{7,3},{8,12},{9,13},{10,... | collective-permute-start | bytes 786440 | tf_op jit(solution)/shard_map/ppermute | solution.py:16
  60.1 15.2 %collective-permute-start.3 = (f32[512,128]{0,1:T(8,128)}, f32[512,128]{0,1:T(8,128)}, u32[]{:S(2)}, u32[]{:S(2)}) collective-permute-start(f32[512,128]{0,1:T(8,128)} %slice_subtract_fusion.3), channel_id=1, source_target_pairs={{0,8},{1,9},{2,10},{3,11},{4,12},{5,13},{6,14},{7,15},{8,0},{9,1},... | collective-permute-start | bytes 786440 | tf_op jit(solution)/shard_map/ppermute | solution.py:16
  68.0 118.0 %all-reduce.7.cloned.1.call-start = ((), (), s32[]{:S(2)}) async-start(), calls=%async_computation.1 | async-start | bytes 917504 | tf_op jit(solution)/shard_map/psum | solution.py:22
  80.4 31.3 %collective-permute-start.4 = (f32[512,128]{0,1:T(8,128)}, f32[512,128]{0,1:T(8,128)}, u32[]{:S(2)}, u32[]{:S(2)}) collective-permute-start(f32[512,128]{0,1:T(8,128)} %slice_subtract_fusion.2), channel_id=1, source_target_pairs={{0,16},{1,17},{2,18},{3,19},{4,20},{5,21},{6,22},{7,23},{8,24},{9,... | collective-permute-start | bytes 786440 | tf_op jit(solution)/shard_map/ppermute | solution.py:16
  111.6 110.4 %all-reduce.11.cloned.1.call-start = ((), (), s32[]{:S(2)}) async-start(), calls=%async_computation.3 | async-start | bytes 917504 | tf_op jit(solution)/shard_map/psum | solution.py:22
  116.8 69.2 %collective-permute-start.5 = (f32[512,128]{0,1:T(8,128)}, f32[512,128]{0,1:T(8,128)S(1)}, u32[]{:S(2)}, u32[]{:S(2)}) collective-permute-start(f32[512,128]{0,1:T(8,128)} %slice_subtract_fusion.1), channel_id=1, source_target_pairs={{0,32},{1,33},{2,34},{3,35},{4,36},{5,37},{6,38},{7,39},{8,40},{9,... | collective-permute-start | bytes 786440 | tf_op jit(solution)/shard_map/ppermute | solution.py:16
  186.0 64.0 %all-gather.2.cloned.1.call-start = ((), (), s32[]{:S(2)}) async-start(), calls=%async_computation | async-start | bytes 1638400 | tf_op jit(solution)/shard_map/all_gather | solution.py:29
  249.9 1.8 slice-start
  251.7 8.8 %copy-start.6 = (f32[128,128]{1,0:T(8,128)S(1)}, f32[128,128]{1,0:T(8,128)}, u32[]{:S(2)}) copy-start(f32[128,128]{1,0:T(8,128)} %get-tuple-element.73) | copy-start | bytes 196612
  260.5 4.6 %copy-start.4 = (f32[6,128,128]{2,1,0:T(8,128)S(1)}, f32[6,128,128]{2,1,0:T(8,128)}, u32[]{:S(2)}) copy-start(f32[6,128,128]{2,1,0:T(8,128)} %get-tuple-element.74) | copy-start | bytes 1179652
Sparse Core Ops, SparseCore 0:
  68.1 43.4 all-reduce.8
  114.0 71.9 all-reduce.6
  188.6 33.3 all-reduce.10
  223.8 26.1 all-gather.1
where the time goes:
time: 279 us; the launch traced here: 276 us
  waiting for transfers between devices  177 us (63%)
  matrix products  61.2 us (22%)
  between operations  14.8 us (5%)
  starting transfers between devices  14 us (5%)
  other arithmetic  5.31 us (2%)
  local copies, waits for them, and re-layouts  3.54 us (1%)
    psum x3, waiting for transfers between devices, from_root(): value = lax.psum(value, axis)  129 us
    dot_general x49, matrix products, product(): return jnp.matmul(left, right, precision=exact_mode)  61.2 us
    all_gather x1, waiting for transfers between devices, in_one_piece(): out = lax.all_gather(both, axis, axis=dim, tiled=True)  26.2 us
    ppermute x6, waiting for transfers between devices, partner_2(): return lax.ppermute(value, axis, pairs)  21.3 us
    ppermute x6, starting transfers between devices, partner_2(): return lax.ppermute(value, axis, pairs)  13.6 us
  transfers between devices with their start and end apart: 10, of which 7 were waited for; matrix products, arithmetic and copies ran while one was open for 10% of the time, Pallas kernels for 0%

commit v1 on v0

v1 whole, which is shorter than its diff:
```python
import jax
import jax.numpy as jnp
from jax import lax
from jax.experimental import pallas as pl
from jax.experimental.pallas import tpu as pltpu
from jax.sharding import Mesh
from jax.sharding import PartitionSpec as P

MESH = pl.DeviceIdType.MESH
BLK = ("blk_0", "blk_1", "blk_2")
BF = jnp.bfloat16
F32 = jnp.float32
NB, RHS, MAP = 16, 32, 8
ROWS = RHS + MAP


def split(value):
    high = value.astype(BF)
    return high, (value - high.astype(F32)).astype(BF)


def dot(left, right):
    return jnp.dot(left, right, preferred_element_type=F32)


def dot3(left, right):
    (lh, ll), (rh, rl) = left, right
    return dot(lh, rh) + (dot(lh, rl) + dot(ll, rh))


def kernel(
    child, x_in, lg_in, li_in, ll_in, ng_in, ni_in, nl_in, cp_in,
    leaf_out, node_out, root_out,
    xb, cp, gen, inv, low, wh, wl,
    sk0, sk1, sk2, sk3, sk4, sk5, rc0, rc1, rc2, rc3, rc4, rc5,
    ag, mr, yin, ynext, inc, mh, ml, ob,
    in_sem, up_s, up_r, z_s, z_r, m_s, m_r, i_s, i_r, d_s, d_r, y_s, y_r, out_sem,
):
    lv = lax.axis_index("level")
    x = lax.axis_index("blk_0")
    z = lax.axis_index("blk_1")
    c = lax.axis_index("blk_2")
    position = (x * 8 + z) * 2 + c
    sk = (sk0, sk1, sk2, sk3, sk4, sk5)
    rc = (rc0, rc1, rc2, rc3, rc4, rc5)

    loads = [
        pltpu.make_async_copy(src, dst, in_sem.at[k])
        for k, (src, dst) in enumerate(
            (
                (lg_in, gen.at[0]),
                (li_in, inv.at[0]),
                (ll_in, low.at[0]),
                (x_in, xb.at[:, pl.ds(0, RHS)]),
                (cp_in, cp),
                (ni_in, inv.at[pl.ds(1, 6)]),
                (nl_in, low.at[pl.ds(1, 6)]),
                (ng_in, gen.at[pl.ds(1, 6)]),
            )
        )
    ]
    for load in loads:
        load.start()

    def bit(value, k):
        return lax.rem(value // (2**k), 2)

    def flipped(value, k):
        out = value
        for j in range(3):
            if k >> j & 1:
                out = out + (1 - 2 * bit(value, j)) * 2**j
        return out

    peer_z = [flipped(z, k) for k in range(8)]
    peer_x = (flipped(x, 1), flipped(x, 2))
    core_peer = (lv, x, z, 1 - c)

    barrier = pltpu.get_barrier_semaphore()

    def greet(device):
        pl.semaphore_signal(barrier, inc=1, device_id=device, device_id_type=MESH)

    greet(core_peer)
    for k in range(1, 8):
        greet((lv, x, peer_z[k], c))
        greet((lv, x, peer_z[k], 1 - c))
    greet((lv, peer_x[0], z, c))
    greet((lv, peer_x[1], z, c))

    @pl.when(lv > 0)
    def _():
        greet((lv - 1, x, z, c))

    @pl.when(lv < 3)
    def _():
        greet((lv + 1, x, z, c))

    def fold(t):
        g_first, g_last = gen[t, :, :128], gen[t, :, 128:]
        first = dot3(split(g_first), split(inv[t]))
        last = g_last - dot3(split(first), split(low[t]))
        high, rest = split(first)
        wh[t, :, :128] = high
        wl[t, :, :128] = rest
        high, rest = split(last)
        wh[t, :, 128:] = high
        wl[t, :, 128:] = rest

    def remote(src, dst, send, recv, device):
        return pltpu.make_async_remote_copy(
            src_ref=src, dst_ref=dst, send_sem=send, recv_sem=recv, device_id=device, device_id_type=MESH
        )

    for k in (0, 1, 2):
        loads[k].wait()
    fold(0)
    loads[3].wait()
    loads[4].wait()
    is_target = child[0] == position
    xb[:, RHS:] = jnp.where(is_target, cp[...], jnp.zeros_like(cp))

    def leaf_chunk(k, carry):
        rows = xb[pl.ds(k * 4, 4)].reshape(4 * ROWS, 256)
        y = dot3(split(rows), (wh[0], wl[0]))
        ag[7, pl.ds(k * 4, 4)] = y[:, :128].reshape(4, ROWS, 128)
        sk0[pl.ds(k * 4, 4)] = y[:, 128:].reshape(4, ROWS, 128)
        return carry

    lax.fori_loop(0, 4, leaf_chunk, 0)

    pl.semaphore_wait(barrier, 17 + jnp.minimum(lv, 1) + jnp.minimum(3 - lv, 1))

    zb = [bit(z, k) for k in range(3)]
    sides = (c, zb[0], zb[1], zb[2], bit(x, 0), bit(x, 1))
    partners = (
        core_peer,
        (lv, x, peer_z[1], c),
        (lv, x, peer_z[2], c),
        (lv, x, peer_z[4], c),
        (lv, peer_x[0], z, c),
        (lv, peer_x[1], z, c),
    )
    starts = [c * 8]
    for h in range(1, 4):
        starts.append(starts[-1] + sides[h] * (8 >> h))
    q = starts[3]
    starts += [q, q]

    def send_z(g, h, blocks, ks):
        out = []
        for k in ks:
            ref = ag.at[h, blocks]
            out.append(remote(ref, ref, z_s.at[g, k], z_r.at[g, k], (lv, x, peer_z[k], c)))
        return out

    def send_core(g, tiers):
        half = ag.at[tiers, pl.ds(c * 8, 8)]
        return remote(half, half, d_s.at[g], d_r.at[g], core_peer)

    relays = [send_core(h, pl.ds(h, 1)) for h in range(4)] + [send_core(4, pl.ds(4, 3))]
    gathers = [
        send_z(0, 1, pl.ds(starts[1], 4), (1,)),
        send_z(1, 2, pl.ds(starts[2], 2), (1, 2, 3)),
        send_z(2, 3, pl.ds(q, 1), range(1, 8)),
    ]
    tops = []
    for k in range(1, 8):
        ref = ag.at[pl.ds(4, 3), pl.ds(q, 1)]
        tops.append(remote(ref, ref, z_s.at[3, k], z_r.at[3, k], (lv, x, peer_z[k], c)))

    ups = []
    for h in range(6):
        side = sides[h]
        count = 8 >> h if h < 4 else 1
        keep = side * count if h < 4 else 0
        give = (1 - side) * count if h < 4 else 0
        up = remote(sk[h].at[pl.ds(give, count)], rc[h], up_s.at[h], up_r.at[h], partners[h])
        up.start()
        ups.append(up)
        if h == 4:
            for group in gathers:
                for copy in group:
                    copy.start()
        if h == 0:
            loads[5].wait()
            loads[6].wait()
            loads[7].wait()
        fold(h + 1)
        up.wait_recv()
        mine_rows = pl.ds(pl.multiple_of(side * 128, 128), 128)
        other_rows = pl.ds(pl.multiple_of((1 - side) * 128, 128), 128)
        step = min(count, 4)
        for k in range(0, count, step):
            mine = sk[h][pl.ds(keep + k, step)].reshape(step * ROWS, 128)
            other = rc[h][pl.ds(k, step)].reshape(step * ROWS, 128)
            y = dot3(split(mine), (wh[h + 1, mine_rows], wl[h + 1, mine_rows]))
            y = y + dot3(split(other), (wh[h + 1, other_rows], wl[h + 1, other_rows]))
            ag[h, pl.ds(starts[h] + k, step)] = y[:, :128].reshape(step, ROWS, 128)
            skeleton = y[:, 128:].reshape(step, ROWS, 128)
            if h < 5:
                sk[h + 1][pl.ds(k, step)] = skeleton
            else:
                ag[6, pl.ds(q, 1)] = skeleton
                mr[pl.ds(q, 1)] = skeleton[:, RHS:]
                ynext[...] = skeleton[:, :RHS]
        if h == 0:
            relays[0].start()

    maps = []
    for k in range(8):
        for side in range(2):
            if k or side:
                ref = mr.at[pl.ds(q, 1)]
                device = (lv, x, peer_z[k], 1 - c if side else c)
                maps.append(remote(ref, ref, m_s.at[2 * k + side], m_r.at[2 * k + side], device))
    for copy in maps:
        copy.start()
    chain = remote(ynext, yin, y_s, y_r, (lv + 1, x, z, c))
    incs = []
    for k in range(1, 8):
        ref = inc.at[pl.ds(q, 1)]
        incs.append(remote(ref, ref, i_s.at[k], i_r.at[k], (lv, x, peer_z[k], c)))
    half = inc.at[pl.ds(c * 8, 8)]
    inc_relay = remote(half, half, d_s.at[5], d_r.at[5], core_peer)

    @pl.when(lv == 0)
    def _():
        chain.start()

    for copy in tops:
        copy.start()
    for g in range(3):
        for copy in gathers[g]:
            copy.wait_recv()
        relays[g + 1].start()
    for copy in maps:
        copy.wait_recv()

    @pl.when(lv == 0)
    def _():
        inc[...] = jnp.zeros_like(inc)

    @pl.when(lv > 0)
    def _():
        chain.wait_recv()
        inc[pl.ds(q, 1)] = yin[...]
        for copy in incs:
            copy.start()

    @pl.when((lv > 0) & (lv < 3))
    def _():
        root_map = mr[...].reshape(128, 128)
        ynext[...] = ynext[...] + dot3(split(yin[...].reshape(RHS, 128)), split(root_map)).reshape(1, RHS, 128)
        chain.start()

    for copy in tops:
        copy.wait_recv()
    relays[4].start()
    for relay in relays:
        relay.wait_recv()

    def split_maps(t, carry):
        high, rest = split(ag[t, :, RHS:].reshape(128, 128))
        mh[t] = high
        ml[t] = rest
        return carry

    lax.fori_loop(0, 8, split_maps, 0)

    @pl.when(lv > 0)
    def _():
        for copy in incs:
            copy.wait_recv()
        inc_relay.start()
        inc_relay.wait_recv()

    def correct(t, carry):
        for k in range(0, NB, 8):
            rows = inc[pl.ds(k, 8)].reshape(8 * RHS, 128)
            update = dot3(split(rows), (mh[t], ml[t]))
            ob[t, pl.ds(k, 8)] = ag[t, pl.ds(k, 8), :RHS] + update.reshape(8, RHS, 128)
        return carry

    lax.fori_loop(0, 8, correct, 0)
    stores = [
        pltpu.make_async_copy(ob.at[pl.ds(0, 6)], node_out, out_sem.at[0]),
        pltpu.make_async_copy(ob.at[6], root_out, out_sem.at[1]),
        pltpu.make_async_copy(ob.at[7], leaf_out, out_sem.at[2]),
    ]
    for store in stores:
        store.start()

    for copy in ups + tops + maps + relays + [copy for group in gathers for copy in group]:
        copy.wait_send()

    @pl.when(lv > 0)
    def _():
        for copy in incs + [inc_relay]:
            copy.wait_send()

    @pl.when(lv < 3)
    def _():
        chain.wait_send()

    for store in stores:
        store.wait()


def shards(
    right_sides, leaf_gen, leaf_inverse, leaf_lower, node_gen, node_inverse, node_lower, coupling, child_leaf
):
    any_space = pl.BlockSpec(memory_space=pl.ANY)
    dma = pltpu.SemaphoreType.DMA
    vm = pltpu.VMEM
    counts = (16, 8, 4, 2, 1, 1)
    leaf, node, root = pl.pallas_call(
        kernel,
        out_shape=(
            jax.ShapeDtypeStruct((NB, RHS, 128), F32),
            jax.ShapeDtypeStruct((6, NB, RHS, 128), F32),
            jax.ShapeDtypeStruct((NB, RHS, 128), F32),
        ),
        in_specs=[pl.BlockSpec(memory_space=pltpu.SMEM)] + [any_space] * 8,
        out_specs=(any_space,) * 3,
        scratch_shapes=[
            vm((NB, ROWS, 256), F32),
            vm((NB, MAP, 256), F32),
            vm((7, 256, 256), F32),
            vm((7, 128, 128), F32),
            vm((7, 128, 128), F32),
            vm((7, 256, 256), BF),
            vm((7, 256, 256), BF),
        ]
        + [vm((n, ROWS, 128), F32) for n in counts]
        + [vm((n, ROWS, 128), F32) for n in (8, 4, 2, 1, 1, 1)]
        + [
            vm((8, NB, ROWS, 128), F32),
            vm((NB, MAP, 128), F32),
            vm((1, RHS, 128), F32),
            vm((1, RHS, 128), F32),
            vm((NB, RHS, 128), F32),
            vm((8, 128, 128), BF),
            vm((8, 128, 128), BF),
            vm((8, NB, RHS, 128), F32),
            dma((8,)),
            dma((6,)),
            dma((6,)),
            dma((4, 8)),
            dma((4, 8)),
            dma((16,)),
            dma((16,)),
            dma((8,)),
            dma((8,)),
            dma((6,)),
            dma((6,)),
            dma,
            dma,
            dma((3,)),
        ],
        compiler_params=pltpu.CompilerParams(
            collective_id=0, has_side_effects=True, vmem_limit_bytes=40 * 1024 * 1024
        ),
    )(
        child_leaf,
        right_sides.reshape(NB, RHS, 256),
        leaf_gen[0],
        leaf_inverse[0],
        leaf_lower[0],
        node_gen[0, 0],
        node_inverse[0, 0],
        node_lower[0, 0],
        coupling.reshape(NB, MAP, 256),
    )
    return (leaf.reshape(1, 512, 128), node.reshape(1, 1, 6, 512, 128), root.reshape(1, 512, 128))


def solution(mesh):
    split_mesh = Mesh(
        mesh.devices.reshape(mesh.shape["level"], 4, 8, 2), ("level", "blk_0", "blk_1", "blk_2")
    )
    return jax.shard_map(
        shards,
        mesh=split_mesh,
        in_specs=(
            P("level", None, BLK),
            P("level", BLK, None),
            P("level", BLK, None),
            P("level", BLK, None),
            P("level", BLK, None, None, None),
            P("level", BLK, None, None, None),
            P("level", BLK, None, None, None),
            P("level", None, None),
            P("level"),
        ),
        out_specs=(
            P("level", None, BLK),
            P("level", BLK, None, None, None),
            P("level", None, None),
        ),
        check_vma=False,
    )
```

time: 279 us -> 67.6 us (0.24); the launches traced: 276 us -> 67.2 us
  waiting for transfers between devices: 177 us -> 0 us
  matrix products: 61.2 us -> 0 us
  Pallas kernels: 0 us -> 55.4 us
  starting transfers between devices: 14 us -> 0 us
  between operations: 14.8 us -> 1.31 us
  local copies, waits for them, and re-layouts: 3.54 us -> 10.5 us
  other arithmetic: 5.31 us -> 0 us
    psum x3 -> x0, waiting for transfers between devices: 129 us -> none  [from_root(): value = lax.psum(value, axis)]
    dot_general x49 -> x0, matrix products: 61.2 us -> none  [product(): return jnp.matmul(left, right, precision=exact_mode)]
    pallas_call x0 -> x1, Pallas kernels: none -> 55.4 us  [shards(): pl.pallas_call(kernel, out_shape=(jax.ShapeDtypeStruct((NB, RHS, 128), F3...]
    all_gather x1 -> x0, waiting for transfers between devices: 26.2 us -> none  [in_one_piece(): out = lax.all_gather(both, axis, axis=dim, tiled=True)]
    ppermute x6 -> x0, waiting for transfers between devices: 21.3 us -> none  [partner_2(): return lax.ppermute(value, axis, pairs)]
    ppermute x6 -> x0, starting transfers between devices: 13.6 us -> none  [partner_2(): return lax.ppermute(value, axis, pairs)]
    unnamed x18 -> x19, local copies, waits for them, and re-layouts: 1.08 us -> 10.5 us
    dynamic_update_slice x4 -> x0, other arithmetic: 2.9 us -> none  [shards(): lax.scan(advance, jnp.zeros((column_total, skeleton_size), jnp.float32),...]
  transfers between devices with their start and end apart: 10 -> 0, of which waited for: 7 -> 0; matrix products, arithmetic and copies ran while one was open for 10% -> 0% of each run, Pallas kernels for 0% -> 0%
where the time goes in v1:
time: 67.6 us; the launch traced here: 67.2 us
  Pallas kernels  55.4 us (82%)
  local copies, waits for them, and re-layouts  10.5 us (16%)
  between operations  1.31 us (2%)
    pallas_call x1, Pallas kernels, shards(): pl.pallas_call(kernel, out_shape=(jax.ShapeDtypeStruct((NB, RHS, 128), F3...  55.4 us
    unnamed x19, local copies, waits for them, and re-layouts  10.5 us

profile of v1, /device:TPU:27, one launch (start us, length us, event | category | flops | bytes accessed | tf_op | source)
XLA Modules:
  0.0 67.2 jit_solution(1979447601599897800)
XLA Ops:
  1.3 0.0 copy-start
  1.3 1.4 %copy-done = f32[1,1,6,256,256]{4,3,2,1,0:T(8,128)S(1)} copy-done((f32[1,1,6,256,256]{4,3,2,1,0:T(8,128)S(1)}, f32[1,1,6,256,256]{4,3,2,1,0:T(8,128)}, u32[]{:S(2)}) %copy-start) | copy-done | bytes 1572888
  2.7 0.0 copy-start.1
  2.7 1.0 %copy-done.1 = f32[1,512,256]{2,1,0:T(8,128)S(1)} copy-done((f32[1,512,256]{2,1,0:T(8,128)S(1)}, f32[1,512,256]{2,1,0:T(8,128)}, u32[]{:S(2)}) %copy-start.1) | copy-done | bytes 524312
  3.7 0.0 copy-start.2
  3.7 1.0 %copy-done.2 = f32[1,1,6,128,128]{4,3,2,1,0:T(8,128)S(1)} copy-done((f32[1,1,6,128,128]{4,3,2,1,0:T(8,128)S(1)}, f32[1,1,6,128,128]{4,3,2,1,0:T(8,128)}, u32[]{:S(2)}) %copy-start.2) | copy-done | bytes 393240
  4.7 0.0 copy-start.3
  4.7 1.0 %copy-done.3 = f32[1,1,6,128,128]{4,3,2,1,0:T(8,128)S(1)} copy-done((f32[1,1,6,128,128]{4,3,2,1,0:T(8,128)S(1)}, f32[1,1,6,128,128]{4,3,2,1,0:T(8,128)}, u32[]{:S(2)}) %copy-start.3) | copy-done | bytes 393240
  5.7 0.0 copy-start.4
  5.7 0.9 %copy-done.4 = f32[1,256,256]{2,1,0:T(8,128)S(1)} copy-done((f32[1,256,256]{2,1,0:T(8,128)S(1)}, f32[1,256,256]{2,1,0:T(8,128)}, u32[]{:S(2)}) %copy-start.4) | copy-done | bytes 262168
  6.7 0.0 copy-start.5
  6.7 0.9 %copy-done.5 = f32[1,128,256]{2,1,0:T(8,128)S(1)} copy-done((f32[1,128,256]{2,1,0:T(8,128)S(1)}, f32[1,128,256]{2,1,0:T(8,128)}, u32[]{:S(2)}) %copy-start.5) | copy-done | bytes 131096
  7.6 0.0 copy-start.6
  7.6 0.8 %copy-done.6 = f32[1,128,128]{2,1,0:T(8,128)S(1)} copy-done((f32[1,128,128]{2,1,0:T(8,128)S(1)}, f32[1,128,128]{2,1,0:T(8,128)}, u32[]{:S(2)}) %copy-start.6) | copy-done | bytes 65560
  8.4 0.0 copy-start.7
  8.4 0.8 %copy-done.7 = f32[1,128,128]{2,1,0:T(8,128)S(1)} copy-done((f32[1,128,128]{2,1,0:T(8,128)S(1)}, f32[1,128,128]{2,1,0:T(8,128)}, u32[]{:S(2)}) %copy-start.7) | copy-done | bytes 65560
  9.3 55.4 %shard_map.112 = (f32[16,32,128]{2,1,0:T(8,128)S(1)}, f32[6,16,32,128]{3,2,1,0:T(8,128)S(1)}, f32[16,32,128]{2,1,0:T(8,128)S(1)}) custom-call(s32[1]{0:T(128)S(6)} %copy.15.child, f32[16,32,256]{2,1,0:T(8,128)S(1)} %bitcast.13, f32[256,256]{1,0:T(8,128)S(1)} %bitcast.16, f32[128,128]{1,0:T(8,128)S(1)} %bitcast.20, f32[128,128]{1,0:T(8,128)S(1)} %bitcast.21, ...), custom_call_target="tpu_custom_call" | custom-call | tf_op jit(solution)/shard_map/pallas_call | solution.py:317
  64.6 0.7 %copy.16 = f32[1,512,128]{2,1,0:T(8,128)} copy(f32[1,512,128]{2,1,0:T(8,128)S(1)} %bitcast.18) | data formatting | bytes 524288
  65.3 1.1 %copy.17 = f32[1,1,6,512,128]{4,3,2,1,0:T(8,128)} copy(f32[1,1,6,512,128]{4,3,2,1,0:T(8,128)S(1)} %bitcast.12) | data formatting | bytes 3145728
  66.5 0.7 %copy.18 = f32[1,512,128]{2,1,0:T(8,128)} copy(f32[1,512,128]{2,1,0:T(8,128)S(1)} %bitcast.17) | data formatting | bytes 524288
Async XLA Ops:
  1.3 1.4 %copy-start = (f32[1,1,6,256,256]{4,3,2,1,0:T(8,128)S(1)}, f32[1,1,6,256,256]{4,3,2,1,0:T(8,128)}, u32[]{:S(2)}) copy-start(f32[1,1,6,256,256]{4,3,2,1,0:T(8,128)} %param.13) | copy-start | bytes 4718596
  2.7 1.0 %copy-start.1 = (f32[1,512,256]{2,1,0:T(8,128)S(1)}, f32[1,512,256]{2,1,0:T(8,128)}, u32[]{:S(2)}) copy-start(f32[1,512,256]{2,1,0:T(8,128)} %param.9) | copy-start | bytes 1572868
  3.7 1.0 %copy-start.2 = (f32[1,1,6,128,128]{4,3,2,1,0:T(8,128)S(1)}, f32[1,1,6,128,128]{4,3,2,1,0:T(8,128)}, u32[]{:S(2)}) copy-start(f32[1,1,6,128,128]{4,3,2,1,0:T(8,128)} %param.14) | copy-start | bytes 1179652
  4.7 1.0 %copy-start.3 = (f32[1,1,6,128,128]{4,3,2,1,0:T(8,128)S(1)}, f32[1,1,6,128,128]{4,3,2,1,0:T(8,128)}, u32[]{:S(2)}) copy-start(f32[1,1,6,128,128]{4,3,2,1,0:T(8,128)} %param.15) | copy-start | bytes 1179652
  5.7 0.9 %copy-start.4 = (f32[1,256,256]{2,1,0:T(8,128)S(1)}, f32[1,256,256]{2,1,0:T(8,128)}, u32[]{:S(2)}) copy-start(f32[1,256,256]{2,1,0:T(8,128)} %param.10) | copy-start | bytes 786436
  6.7 0.9 %copy-start.5 = (f32[1,128,256]{2,1,0:T(8,128)S(1)}, f32[1,128,256]{2,1,0:T(8,128)}, u32[]{:S(2)}) copy-start(f32[1,128,256]{2,1,0:T(8,128)} %param.16) | copy-start | bytes 393220
  7.6 0.8 %copy-start.6 = (f32[1,128,128]{2,1,0:T(8,128)S(1)}, f32[1,128,128]{2,1,0:T(8,128)}, u32[]{:S(2)}) copy-start(f32[1,128,128]{2,1,0:T(8,128)} %param.11) | copy-start | bytes 196612
  8.4 0.8 %copy-start.7 = (f32[1,128,128]{2,1,0:T(8,128)S(1)}, f32[1,128,128]{2,1,0:T(8,128)}, u32[]{:S(2)}) copy-start(f32[1,128,128]{2,1,0:T(8,128)} %param.12) | copy-start | bytes 196612
